TPU v7x, 32 devices: a 4x4x1 block of a 4x4x8 slice. The times are simulated.
32 devices in a mesh: dp: 1 (over z), tp: 4 (over y), ep: 8 (over x, core).
Axes of the slice: x: 4, y: 4, z: 1, core: 2. Of those that a mesh axis runs over, the one named last changes fastest.
The devices are a block of a 4x4x8 slice.
Arguments:
- hidden: bfloat16 [16384, 2048], P(('dp', 'ep'))
- expert_ids: int32 [16384, 2], P(('dp', 'ep'))
- norm_w: bfloat16 [2048], replicated
- router_w: bfloat16 [2048, 8], replicated
- w_gate: bfloat16 [8, 2048, 5632], P('ep', None, 'tp')
- w_up: bfloat16 [8, 2048, 5632], P('ep', None, 'tp')
- w_down: bfloat16 [8, 5632, 2048], P('ep', 'tp')
Outputs:
- output: bfloat16 [16384, 2048], P(('dp', 'ep'))
All inputs are finite; a program needn't handle non-finite values.
Results may differ from a plain program's by a relative error of at most 0.0106688.
Values are sent between devices in bfloat16 or wider.
A program may use at most 768 MiB of HBM per device.

v0:
```python
import jax
import jax.numpy as jnp
from jax import lax
from jax.sharding import PartitionSpec as P

NORM_EPS = 1e-6


def rms_norm(hidden, norm_w):
    wide_h = hidden.astype(jnp.float32)
    mean_sq = jnp.mean(wide_h * wide_h, axis=-1, keepdims=True)
    return (wide_h * lax.rsqrt(mean_sq + NORM_EPS) * norm_w.astype(jnp.float32)).astype(jnp.bfloat16)


def slot_rank(expert_ids, n_experts):
    flat_ids = expert_ids.reshape(-1)
    one_hot = (flat_ids[:, None] == jnp.arange(n_experts, dtype=jnp.int32)[None, :]).astype(jnp.int32)
    running = jnp.cumsum(one_hot, axis=0)
    return jnp.sum(running * one_hot, axis=1) - 1


def row_cap(tok_dev, top_k, n_experts):
    return 8 * ((2 * top_k * tok_dev + 8 * n_experts - 1) // (8 * n_experts))


def gather_slots(normed, slot_dest, n_slots, top_k):
    pair_tok = jnp.arange(slot_dest.shape[0], dtype=jnp.int32) // top_k
    src_tok = jnp.zeros((n_slots,), jnp.int32).at[slot_dest].set(pair_tok)
    filled = jnp.zeros((n_slots,), jnp.int32).at[slot_dest].set(1)
    return jnp.where(filled[:, None] > 0, normed[src_tok], jnp.zeros((), jnp.bfloat16))


def solution(mesh):
    ep_size = mesh.shape["ep"]

    def per_device(hidden, expert_ids, norm_w, router_w, w_gate, w_up, w_down):
        tok_dev, model_dim = hidden.shape
        top_k = expert_ids.shape[1]
        n_experts = router_w.shape[1]
        local_exp = w_gate.shape[0]
        row_limit = row_cap(tok_dev, top_k, n_experts)
        n_slots = n_experts * row_limit
        normed = rms_norm(hidden, norm_w)
        logits = jnp.dot(normed, router_w, preferred_element_type=jnp.float32)
        gate_prob = jnp.take_along_axis(jax.nn.softmax(logits, axis=-1), expert_ids, axis=-1)
        slot_dest = expert_ids.reshape(-1) * row_limit + slot_rank(expert_ids, n_experts)
        send_rows = gather_slots(normed, slot_dest, n_slots, top_k).reshape(ep_size, local_exp, row_limit, model_dim)
        recv_rows = lax.all_to_all(send_rows, "ep", 0, 2, tiled=True).reshape(local_exp, ep_size * row_limit, model_dim)
        gate_pre = jnp.einsum("erd,edf->erf", recv_rows, w_gate, preferred_element_type=jnp.float32)
        up_pre = jnp.einsum("erd,edf->erf", recv_rows, w_up, preferred_element_type=jnp.float32)
        act_rows = (jax.nn.silu(gate_pre) * up_pre).astype(jnp.bfloat16)
        part_out = jnp.einsum("erf,efd->erd", act_rows, w_down, preferred_element_type=jnp.float32).astype(jnp.bfloat16)
        expert_out = lax.psum(part_out, "tp")
        back_rows = lax.all_to_all(expert_out.reshape(1, local_exp, ep_size * row_limit, model_dim), "ep", 2, 0, tiled=True)
        picked = back_rows.reshape(n_slots, model_dim)[slot_dest].reshape(tok_dev, top_k, model_dim)
        moe_sum = jnp.sum(picked.astype(jnp.float32) * gate_prob[:, :, None], axis=1)
        return (hidden.astype(jnp.float32) + moe_sum).astype(jnp.bfloat16)

    token_spec = P(("dp", "ep"), None)
    return jax.shard_map(per_device, mesh=mesh, in_specs=(token_spec, token_spec, P(None), P(None, None), P("ep", None, "tp"), P("ep", None, "tp"), P("ep", "tp", None)), out_specs=token_spec, check_vma=False)
```

profile of v0, /device:TPU:97, one launch (start us, length us, event | category | flops | bytes accessed | tf_op | source)
XLA Modules:
  0.0 2244.9 jit_solution(10667234393640770208)
XLA Ops:
  6.5 0.0 copy-start
  6.6 0.7 broadcast_multiply_fusion
  7.3 1.1 copy.38
  8.4 0.5 eq.29
  8.8 0.5 eq.25
  9.3 0.7 convert_element_type.36
  10.0 5.1 fusion
  15.1 0.4 copy.37
  15.5 0.6 mul.57
  16.1 2.3 reduce-window.6
  18.4 0.3 slice_reduce_fusion
  18.8 0.2 reduce-window.9
  18.9 0.1 add_bitcast_fusion
  19.0 0.1 fusion.10
  19.2 0.0 copy-start.4
  19.2 15.5 scatter_custom_fusion.1
  34.8 15.5 scatter_custom_fusion
  50.4 8.7 fusion.2
  59.1 65.8 %gather_fusion = bf16[8192,2048]{1,0:T(8,128)(2,1)} fusion(bf16[2048,2048]{1,0:T(8,128)(2,1)} %fusion.2, s32[8192]{0:T(1024)S(1)} %fusion.14), kind=kCustom, calls=%fused_computation | custom fusion | bytes 67141632 | tf_op jit(solution)/shard_map/gather | solution.py:30
  124.9 23.3 %broadcast_select_fusion = bf16[8,1,1024,2048]{3,2,1,0:T(8,128)(2,1)} fusion(bf16[8,1,1024,2048]{3,2,1,0:T(8,128)(2,1)} %bitcast.60, pred[8,1024]{1,0:T(8,128)(4,1)S(1)} %broadcast_in_dim.20), kind=kLoop, calls=%fused_computation.9 | loop fusion | flops 16777216 | bytes 67117056 | tf_op jit(solution)/shard_map/jit(_where)/select_n | solution.py:30
  148.3 377.1 %all_to_all.8 = bf16[8,1,1024,2048]{3,2,1,0:T(8,128)(2,1)} all-to-all(bf16[8,1,1024,2048]{3,2,1,0:T(8,128)(2,1)} %broadcast_select_fusion), channel_id=1, replica_groups=mesh['dp'=1,'tp'=4,'ep'=8] {'ep'}, dimensions={0} | all-to-all | bytes 67108864 | tf_op jit(solution)/shard_map/all_to_all | solution.py:48
  525.4 60.9 %fusion.7 = f32[8192,1408]{1,0:T(8,128)} fusion(bf16[8192,2048]{1,0:T(8,128)(2,1)} %bitcast.61, bf16[1,2048,1408]{2,1,0:T(8,128)(2,1)} %param.11), kind=kOutput, calls=%fused_computation.19 | convolution fusion | flops 47244640256 | bytes 85458944 | tf_op jit(solution)/shard_map/erd,edf->erf/dot_general | solution.py:49
  586.3 64.3 %multiply_convert_fusion.clone.4 = bf16[8192,1408]{1,0:T(8,128)(2,1)} fusion(f32[8192,1408]{1,0:T(8,128)} %fusion.7, bf16[8192,2048]{1,0:T(8,128)(2,1)} %bitcast.62, bf16[1,2048,1408]{2,1,0:T(8,128)(2,1)S(1)} %bitcast.69), kind=kOutput, calls=%fused_computation.5.clone.clone.clone.1 | convolution fusion | flops 47313846272 | bytes 108527616 | tf_op jit(solution)/shard_map/erd,edf->erf/dot_general | solution.py:50
  650.7 59.0 %convert_bitcast_fusion = bf16[1,1,8192,2048]{3,2,1,0:T(8,128)(2,1)} fusion(bf16[1,1408,2048]{2,1,0:T(8,128)(2,1)} %param.13, bf16[8192,1408]{1,0:T(8,128)(2,1)} %multiply_convert_fusion.clone.4), kind=kOutput, calls=%fused_computation.8 | convolution fusion | flops 47261417472 | bytes 62390272 | tf_op jit(solution)/shard_map/erf,efd->erd/dot_general | solution.py:52
  709.7 0.1 all-reduce.2.cloned.1.call-update
  709.7 560.7 %all-reduce.2.cloned.1.call-done = bf16[1,1,8192,2048]{3,2,1,0:T(8,128)(2,1)} async-done(((bf16[1,1,8192,2048]{3,2,1,0:T(8,128)(2,1)}), bf16[1,1,8192,2048]{3,2,1,0:T(8,128)(2,1)}) %all-reduce.2.cloned.1.call-update) | async-done | bytes 33554448 | tf_op jit(solution)/shard_map/psum | solution.py:53
  1270.4 56.6 %copy.51 = bf16[1,1,8192,2048]{3,1,0,2:T(2,128)(2,1)} copy(bf16[1,1,8192,2048]{3,2,1,0:T(8,128)(2,1)} %all-reduce.2.cloned.1.call-done) | data formatting | bytes 67108864 | tf_op jit(solution)/shard_map/psum | solution.py:53
  1327.1 0.6 broadcast.164
  1327.6 196.0 %reduce.2 = bf16[8192,2048]{1,0:T(8,128)(2,1)} reduce(bf16[8192,1,1,2048]{3,2,1,0:T(2,128)(2,1)} %bitcast.55, bf16[]{:T(256)} %broadcast.164), dimensions={1,2}, to_apply=%bitcast.55.reduce_sub_computation | reduce | bytes 67108864
  1523.6 30.7 %reshape.198 = bf16[8,2,1048576]{2,1,0:T(2,128)(2,1)} reshape(bf16[8192,2048]{1,0:T(8,128)(2,1)} %reduce.2) | data formatting | bytes 67108864
  1554.3 8.4 all-to-all-start.1
  1562.8 0.4 copy.42
  1563.2 0.5 reshape.165
  1563.7 5.7 fusion.23
  1569.4 0.0 copy-start.3
  1569.4 24.5 %gather_fusion.2 = f32[4096]{0:T(1024)S(1)} fusion(f32[2048,8]{0,1:T(8,128)S(1)} %fusion.12, s32[4096]{0:T(1024)S(1)} %reshape.165), kind=kCustom, calls=%fused_computation.2 | custom fusion | bytes 65536 | tf_op jit(solution)/shard_map/jit(take_along_axis)/gather | solution.py:45
  1594.0 1.0 reshape.168
  1595.0 0.3 copy.43
  1595.3 0.0 copy-done.3
  1595.3 0.4 copy.44
  1595.7 330.2 %all-to-all-done.1 = bf16[8,2,1048576]{2,1,0:T(2,128)(2,1)} async-done(((bf16[8,2,1048576]{2,1,0:T(2,128)(2,1)}), bf16[8,2,1048576]{2,1,0:T(2,128)(2,1)}, u32[]{:S(2)}, u32[]{:S(2)}) %all-to-all-start.1) | async-done | bytes 33554464 | tf_op jit(solution)/shard_map/all_to_all | solution.py:54
  1925.9 71.2 %reshape.199 = bf16[8192,1,1,2048]{3,2,1,0:T(2,128)(2,1)} reshape(bf16[8,2,1048576]{2,1,0:T(2,128)(2,1)} %all-to-all-done.1) | data formatting | bytes 67108864
  1997.1 41.1 %copy.50 = bf16[1,1,8192,2048]{3,2,0,1:T(8,128)(2,1)} copy(bf16[1,1,8192,2048]{3,1,0,2:T(2,128)(2,1)} %bitcast.39) | data formatting | bytes 67108864
  2038.2 95.7 %gather_fusion.1 = bf16[4096,2048]{1,0:T(8,128)(2,1)} fusion(bf16[8192,2048]{1,0:T(8,128)(2,1)} %bitcast.59, s32[4096]{0:T(1024)S(1)} %broadcast_clamp_fusion), kind=kCustom, calls=%fused_computation.1 | custom fusion | bytes 33570816 | tf_op jit(solution)/shard_map/gather | solution.py:55
  2133.9 35.3 %reshape.148 = f32[2048,2,2048]{2,1,0:T(2,128)} reshape(bf16[4096,2048]{1,0:T(8,128)(2,1)} %gather_fusion.1) | data formatting | bytes 50331648 | tf_op jit(solution)/shard_map/convert_element_type | solution.py:56
  2169.2 0.0 copy-start.1
  2169.2 56.3 %multiply_reduce_fusion = f32[2048,2048]{1,0:T(8,128)} fusion(f32[2048,2,2048]{2,1,0:T(2,128)} %reshape.148, f32[2048,2]{1,0:T(8,128)S(1)} %copy.44), kind=kLoop, calls=%fused_computation.7 | loop fusion | flops 12582912 | bytes 50348032 | tf_op jit(solution)/shard_map/reduce_sum | solution.py:56
  2225.5 12.0 fusion.3
  (27 shorter events, 0.2 us)
Async XLA Ops:
  6.5 1557.1 %copy-start = (bf16[2048,8]{0,1:T(8,128)(2,1)S(1)}, bf16[2048,8]{0,1:T(8,128)(2,1)}, u32[]{:S(2)}) copy-start(bf16[2048,8]{0,1:T(8,128)(2,1)} %param.10) | copy-start | bytes 98308
  6.6 1263.9 %all-reduce.2.cloned.1.call-start = ((), (), s32[]{:S(2)}) async-start(), calls=%async_computation.2 | async-start | bytes 67108864 | tf_op jit(solution)/shard_map/psum | solution.py:53
  19.2 105.7 %copy-start.4 = (s32[4096,1]{0,1:T(1,128)}, s32[4096,1]{0,1:T(1,128)S(1)}, u32[]{:S(2)}) copy-start(s32[4096,1]{0,1:T(1,128)S(1)} %compare_select_fusion) | copy-start | bytes 49156
  148.3 438.0 %slice-start = ((s8[5767168]{0:T(1024)(128)(4,1)}), s8[4194304]{0:T(1024)(128)(4,1)S(1)}, s32[]{:S(2)}) async-start(s8[5767168]{0:T(1024)(128)(4,1)} %bitcast.68), calls=%async_computation.3 | async-start | bytes 8388608
  525.4 60.9 %slice-start.1 = ((s8[5767168]{0:T(1024)(128)(4,1)}), s8[1572864]{0:T(1024)(128)(4,1)S(1)}, s32[]{:S(2)}) async-start(s8[5767168]{0:T(1024)(128)(4,1)} %bitcast.68), calls=%async_computation.4 | async-start | bytes 3145728
  1554.3 8.5 copy-start.2
  1554.3 371.6 %all-to-all-start.1 = ((bf16[8,2,1048576]{2,1,0:T(2,128)(2,1)}), bf16[8,2,1048576]{2,1,0:T(2,128)(2,1)}, u32[]{:S(2)}, u32[]{:S(2)}) async-start(bf16[8,2,1048576]{2,1,0:T(2,128)(2,1)} %reshape.198), calls=%async_computation.1 | async-start | bytes 67108864 | tf_op jit(solution)/shard_map/all_to_all | solution.py:54
  1569.4 25.9 %copy-start.3 = (s32[2048,2]{0,1:T(2,128)S(1)}, s32[2048,2]{0,1:T(2,128)}, u32[]{:S(2)}) copy-start(s32[2048,2]{0,1:T(2,128)} %param.8) | copy-start | bytes 49156
  1569.4 26.3 %copy-start.5 = (s32[4096,1]{0,1:T(1,128)S(1)}, s32[4096,1]{0,1:T(1,128)}, u32[]{:S(2)}) copy-start(s32[4096,1]{0,1:T(1,128)} %copy-done.4) | copy-start | bytes 49156
  2169.2 68.3 %copy-start.1 = (bf16[2048,8]{0,1:T(8,128)(2,1)S(1)}, bf16[2048,8]{0,1:T(8,128)(2,1)}, u32[]{:S(2)}) copy-start(bf16[2048,8]{0,1:T(8,128)(2,1)} %param.10) | copy-start | bytes 98308
Sparse Core Ops, SparseCore 0:
  709.8 560.5 all-reduce.1
where the time goes:
time: 2260 us; the launch traced here: 2240 us
  waiting for transfers between devices  891 us (39%)
  local copies, waits for them, and re-layouts  459 us (20%)
  blocking collectives  377 us (17%)
  other arithmetic  306 us (14%)
  matrix products  190 us (8%)
    psum x1, waiting for transfers between devices, per_device(): expert_out = lax.psum(part_out, 'tp')  561 us
    all_to_all x1, blocking collectives, per_device(): lax.all_to_all(send_rows, 'ep', 0, 2, tiled=True)  377 us
    all_to_all x1, waiting for transfers between devices, per_device(): lax.all_to_all(expert_out.reshape(1, local_exp, ep_size * row_limit, mode...  330 us
    unnamed x3, other arithmetic  196 us
    unnamed x21, local copies, waits for them, and re-layouts  145 us
    gather x1, local copies, waits for them, and re-layouts, per_device(): back_rows.reshape(n_slots, model_dim)[slot_dest]  95.7 us
    gather x1, local copies, waits for them, and re-layouts, gather_slots(): normed[src_tok]  65.8 us
    dot_general x1, matrix products, per_device(): jnp.einsum('erd,edf->erf', recv_rows, w_up, preferred_element_type=jnp.fl...  64.3 us
  transfers between devices with their start and end apart: 2, of which 2 were waited for; matrix products, arithmetic and copies ran while one was open for 1% of the time, Pallas kernels for 0%

commit v1 on v0

v1 whole, which is shorter than its diff:
```python
import functools

import jax
import jax.numpy as jnp
from jax import lax
from jax.experimental import pallas as pl
from jax.experimental.pallas import tpu as pltpu
from jax.sharding import PartitionSpec as P

NORM_EPS = 1e-6
VMEM_LIMIT = 60 * 1024 * 1024
SLOT_TILE = 256
TOK_TILE = 512
RING = 4
MESH = pl.DeviceIdType.MESH
BLOCKS = ((0, 0), (0, 1), (-1, 0), (1, 0), (-1, 1), (1, 1), (2, 0), (2, 1))


def rms_norm(hidden, norm_w):
    wide_h = hidden.astype(jnp.float32)
    mean_sq = jnp.mean(wide_h * wide_h, axis=-1, keepdims=True)
    return (wide_h * lax.rsqrt(mean_sq + NORM_EPS) * norm_w.astype(jnp.float32)).astype(jnp.bfloat16)


def row_cap(tok_dev, top_k, n_experts):
    return 8 * ((2 * top_k * tok_dev + 8 * n_experts - 1) // (8 * n_experts))


def expert_kernel(chips, tp_size, v_ref, pos_ref, gate_hbm, up_hbm, down_hbm, vbuf, home,
                  gate_ref, up_ref, down_ref, v_now, pos_now, stage, recv_f, recv_c, recv_d, fin,
                  w_sem, v_sem, part_sem, hop_send, hop_recv, pair_send, pair_recv, fwd_send, fwd_recv,
                  f_send, f_recv, c_send, c_recv, d_send, d_recv, home_send, home_recv, own_sem):
    y = lax.axis_index("tp")
    me = lax.axis_index("ep")
    chip, core = me // 2, me % 2
    tok_dev = v_ref.shape[0]
    half, quarter = tok_dev // 2, tok_dev // 4
    n_tiles = home.shape[1] // SLOT_TILE
    steps = len(BLOCKS) * n_tiles
    wide = v_now.shape[1] // tp_size
    side = wide // 2
    to_ep = lambda dx, c: {"ep": 2 * lax.rem(chip + dx + chips, chips) + c}
    to_tp = lambda dy: {"tp": lax.rem(y + dy + tp_size, tp_size)}
    partner = to_ep(0, 1 - core)

    weights = [pltpu.make_async_copy(a, b, w_sem.at[j]) for j, (a, b) in enumerate(((gate_hbm, gate_ref), (up_hbm, up_ref), (down_hbm, down_ref)))]
    for w in weights:
        w.start()

    barrier = pltpu.get_barrier_semaphore()
    peers = [to_tp(1), to_tp(-1), partner] + [to_ep(dx, c) for dx in (-1, 1, 2) for c in (0, 1)]
    for peer in peers:
        pl.semaphore_signal(barrier, inc=1, device_id=peer, device_id_type=MESH)
    pl.semaphore_wait(barrier, len(peers))

    def remote(src, dst, send, recv, device):
        return pltpu.make_async_remote_copy(src_ref=src, dst_ref=dst, send_sem=send, recv_sem=recv, device_id=device, device_id_type=MESH)

    mine = pl.ds(pl.multiple_of(core * half, half), half)
    others = pl.ds(pl.multiple_of((1 - core) * half, half), half)

    def swap(j):
        rows = others if j == 0 else mine
        return remote(v_ref.at[rows], vbuf.at[0, rows], part_sem.at[0, j], part_sem.at[1, j], partner)

    def hop(sc, sign, own):
        src = v_ref.at[mine] if own else vbuf.at[0, mine]
        k = BLOCKS.index((-sign, sc)) - 1
        return remote(src, vbuf.at[k, mine], hop_send.at[sc, (sign + 1) // 2], hop_recv.at[sc, (sign + 1) // 2], to_ep(sign, core))

    def forward(sc, sign):
        rows = pl.ds(pl.multiple_of(core * half + (quarter if sign < 0 else 0), quarter), quarter)
        return remote(vbuf.at[BLOCKS.index((-sign, sc)) - 1, rows], vbuf.at[BLOCKS.index((2, sc)) - 1, rows], fwd_send.at[sc, (sign + 1) // 2], fwd_recv.at[sc, (sign + 1) // 2], to_ep(sign, core))

    def pair(k):
        return remote(vbuf.at[k - 1, mine], vbuf.at[k - 1, mine], pair_send.at[k], pair_recv.at[k], partner)

    def pair_arrival(k):
        return remote(vbuf.at[k - 1, others], vbuf.at[k - 1, others], pair_send.at[k], pair_recv.at[k], partner)

    swap(0).start()
    swap(1).start()

    @pl.when(core == 0)
    def _():
        hop(0, 1, True).start()
        hop(0, -1, True).start()

    @pl.when(core == 1)
    def _():
        remote(v_ref.at[mine], vbuf.at[0, mine], part_sem.at[0, 0], part_sem.at[1, 0], partner).wait_recv()
        hop(0, 1, False).start()
        hop(0, -1, False).start()
        hop(1, 1, True).start()
        hop(1, -1, True).start()

    @pl.when(core == 0)
    def _():
        remote(v_ref.at[mine], vbuf.at[0, mine], part_sem.at[0, 0], part_sem.at[1, 0], partner).wait_recv()
        hop(1, 1, False).start()
        hop(1, -1, False).start()

    def load(src, row):
        copy = pltpu.make_async_copy(src, v_now, v_sem)
        copy.start()
        pos_now[...] = pos_ref[pl.ds(row, 1), :]
        copy.wait()

    def block_start(k):
        dx, sc = BLOCKS[k]
        if k == 0:
            for w in weights:
                w.wait()
            load(v_ref, me)
            return
        if k == 1:
            remote(v_ref.at[others], vbuf.at[0, others], part_sem.at[0, 1], part_sem.at[1, 1], partner).wait_recv()
            load(vbuf.at[0], 2 * chip + 1 - core)
            return
        if k in (2, 4):
            for sign in (1, -1):
                hop(sc, sign, True).wait_recv()
                forward(sc, sign).start()
                pair(BLOCKS.index((-sign, sc))).start()
        if dx == 2:
            for sign in (1, -1):
                forward(sc, sign).wait_recv()
            pair(k).start()
        pair_arrival(k).wait_recv()
        load(vbuf.at[k - 1], 2 * lax.rem(chip + dx + chips, chips) + sc)

    def f_copy(s, d):
        return remote(stage.at[s, 3, d], recv_f.at[d, s], f_send.at[d, s], f_recv.at[d, s], to_tp(1 - 2 * d))

    def c_copy(s, d):
        return remote(stage.at[s, 1 + d, d], recv_c.at[d, s], c_send.at[d, s], c_recv.at[d, s], to_tp(1 - 2 * d))

    def d_copy(s, d):
        return remote(stage.at[s, 1 + d, 1 - d], recv_d.at[d, s], d_send.at[d, s], d_recv.at[d, s], to_tp(1 - 2 * d))

    def rows_of(tile):
        return pl.ds(pl.multiple_of(tile * SLOT_TILE, SLOT_TILE), SLOT_TILE)

    def home_copy(k, s, tile):
        dx, sc = BLOCKS[k]
        device = partner if k == 1 else to_ep(dx, sc)
        return remote(fin.at[s], home.at[me, rows_of(tile)], home_send.at[s], home_recv, device)

    def own_copy(s, tile):
        return pltpu.make_async_copy(fin.at[s], home.at[me, rows_of(tile)], own_sem.at[s])

    def step(i, carry):
        for k in range(len(BLOCKS)):
            @pl.when(i == k * n_tiles)
            def _(k=k):
                block_start(k)

        @pl.when(i < steps)
        def _():
            s = lax.rem(i, RING)

            @pl.when(i >= RING)
            def _():
                for d in (0, 1):
                    f_copy(s, d).wait_send()
                    c_copy(s, d).wait_send()
                    d_copy(s, d).wait_send()

            slots = lax.rem(i, n_tiles) * SLOT_TILE + lax.broadcasted_iota(jnp.int32, (SLOT_TILE, tok_dev), 0)
            pick = jnp.where(pos_now[...] == slots, 1.0, 0.0).astype(jnp.bfloat16)
            rows = jnp.dot(pick, v_now[...], preferred_element_type=jnp.float32).astype(jnp.bfloat16)
            gate_pre = jnp.dot(rows, gate_ref[...], preferred_element_type=jnp.float32)
            up_pre = jnp.dot(rows, up_ref[...], preferred_element_type=jnp.float32)
            act = (jax.nn.silu(gate_pre) * up_pre).astype(jnp.bfloat16)
            for part, dy in ((3, 2), (1, 1), (2, -1), (0, 0)):
                q = lax.rem(y + dy + tp_size, tp_size)
                for d in (0, 1):
                    cols = pl.ds(pl.multiple_of(q * wide + d * side, side), side)
                    stage[s, part, d] = jnp.dot(act, down_ref[:, cols], preferred_element_type=jnp.float32).astype(jnp.bfloat16)
            for d in (0, 1):
                f_copy(s, d).start()
            for d in (0, 1):
                d_copy(s, d).start()

        @pl.when(i >= 2)
        def _():
            j = i - 2
            s = lax.rem(j, RING)
            tile = lax.rem(j, n_tiles)
            for d in (0, 1):
                c_copy(s, d).wait_recv()
                d_copy(s, d).wait_recv()

            @pl.when((j >= RING) & (j < RING + n_tiles))
            def _():
                own_copy(s, tile).wait()

            @pl.when(j >= RING + n_tiles)
            def _():
                home_copy(2, s, tile).wait_send()

            f32 = lambda a: a.astype(jnp.float32)
            for d in (0, 1):
                total = f32(stage[s, 0, d]) + f32(recv_c[d, s]) + f32(recv_d[1 - d, s])
                fin[s, :, d * side:(d + 1) * side] = total.astype(jnp.bfloat16)

            @pl.when(j < n_tiles)
            def _():
                own_copy(s, tile).start()

            for k in range(1, len(BLOCKS)):
                @pl.when(j // n_tiles == k)
                def _(k=k):
                    home_copy(k, s, tile).start()

        @pl.when((i >= 1) & (i <= steps))
        def _():
            s = lax.rem(i - 1, RING)
            for d in (0, 1):
                f_copy(s, d).wait_recv()
                stage[s, 1 + d, d] = (stage[s, 1 + d, d].astype(jnp.float32) + recv_f[d, s].astype(jnp.float32)).astype(jnp.bfloat16)
                c_copy(s, d).start()

        return carry

    assert n_tiles == RING
    lax.fori_loop(0, steps + 2, step, 0)

    for s in range(RING):
        for d in (0, 1):
            f_copy(s, d).wait_send()
            c_copy(s, d).wait_send()
            d_copy(s, d).wait_send()
        home_copy(2, s, s).wait_send()
    for j in (0, 1):
        swap(j).wait_send()
    for sc in (0, 1):
        for sign in (1, -1):
            hop(sc, sign, True).wait_send()
            forward(sc, sign).wait_send()
    for k in range(2, len(BLOCKS)):
        pair(k).wait_send()
    arrived = home.at[pl.ds(0, home.shape[0] - 1)]
    remote(arrived, arrived, home_send.at[0], home_recv, partner).wait_recv()


def experts_apply(chips, tp_size, row_limit, v, pos_rows, gate, up, down):
    tok_dev, dim = v.shape
    ff = gate.shape[1]
    width = dim // tp_size
    side = width // 2
    n = len(BLOCKS)
    bf16 = jnp.bfloat16
    anywhere = pl.BlockSpec(memory_space=pl.ANY)
    dma = pltpu.SemaphoreType.DMA
    ring = (2, RING, SLOT_TILE, side)
    return pl.pallas_call(
        functools.partial(expert_kernel, chips, tp_size),
        out_shape=(jax.ShapeDtypeStruct((n - 1, tok_dev, dim), bf16), jax.ShapeDtypeStruct((n, row_limit, width), bf16)),
        in_specs=[anywhere, pl.BlockSpec(memory_space=pltpu.VMEM), anywhere, anywhere, anywhere],
        out_specs=(anywhere, anywhere),
        scratch_shapes=[
            pltpu.VMEM((dim, ff), bf16), pltpu.VMEM((dim, ff), bf16), pltpu.VMEM((ff, dim), bf16),
            pltpu.VMEM((tok_dev, dim), bf16), pltpu.VMEM((1, tok_dev), jnp.int32),
            pltpu.VMEM((RING, 4, 2, SLOT_TILE, side), bf16), pltpu.VMEM(ring, bf16), pltpu.VMEM(ring, bf16), pltpu.VMEM(ring, bf16),
            pltpu.VMEM((RING, SLOT_TILE, width), bf16),
            dma((3,)), dma, dma((2, 2)), dma((2, 2)), dma((2, 2)), dma((n,)), dma((n,)), dma((2, 2)), dma((2, 2)),
            dma((2, RING)), dma((2, RING)), dma((2, RING)), dma((2, RING)), dma((2, RING)), dma((2, RING)),
            dma((RING,)), dma, dma((RING,)),
        ],
        cost_estimate=pl.CostEstimate(flops=2 * n * row_limit * dim * (tok_dev + 3 * ff), bytes_accessed=2 * (n * tok_dev * dim + 3 * dim * ff), transcendentals=n * row_limit * ff),
        compiler_params=pltpu.CompilerParams(collective_id=0, has_side_effects=True, vmem_limit_bytes=VMEM_LIMIT),
        name="experts",
    )(v, pos_rows, gate, up, down)[1]


def combine_kernel(hidden_ref, pos_ref, prob_ref, y_ref, out_ref):
    acc = hidden_ref[...].astype(jnp.float32)
    for e in range(y_ref.shape[0]):
        slots = lax.broadcasted_iota(jnp.int32, (acc.shape[0], y_ref.shape[1]), 1)
        pick = jnp.where(pos_ref[:, e:e + 1] == slots, 1.0, 0.0).astype(jnp.bfloat16)
        acc += prob_ref[:, e:e + 1] * jnp.dot(pick, y_ref[e], preferred_element_type=jnp.float32)
    out_ref[...] = acc.astype(out_ref.dtype)


def combine(hidden, pos, probs, y, column):
    toks, dim = hidden.shape
    n, limit, width = y.shape
    return pl.pallas_call(
        combine_kernel,
        out_shape=jax.ShapeDtypeStruct((toks, width), hidden.dtype),
        grid=(toks // TOK_TILE,),
        in_specs=[pl.BlockSpec((TOK_TILE, width), lambda i: (i, 0)), pl.BlockSpec((TOK_TILE, n), lambda i: (i, 0)), pl.BlockSpec((TOK_TILE, n), lambda i: (i, 0)),
                  pl.BlockSpec((n, limit, width), lambda i: (0, 0, 0), pipeline_mode=pl.Buffered(1))],
        out_specs=pl.BlockSpec((TOK_TILE, width), lambda i: (i, 0)),
        cost_estimate=pl.CostEstimate(flops=2 * toks * limit * width * n, bytes_accessed=2 * n * limit * width + 8 * toks * width, transcendentals=0),
        compiler_params=pltpu.CompilerParams(vmem_limit_bytes=VMEM_LIMIT),
        name="combine",
    )(lax.dynamic_slice_in_dim(hidden, column * width, width, axis=1), pos, probs, y)


def solution(mesh):
    chips = mesh.shape["ep"] // 2
    tp_size = mesh.shape["tp"]

    def per_device(hidden, expert_ids, norm_w, router_w, w_gate, w_up, w_down):
        tok_dev = hidden.shape[0]
        top_k = expert_ids.shape[1]
        n_experts = router_w.shape[1]
        row_limit = row_cap(tok_dev, top_k, n_experts)
        experts = jnp.arange(n_experts, dtype=jnp.int32)
        chosen = jnp.sum((expert_ids[:, :, None] == experts).astype(jnp.int32), axis=1)
        pos = jnp.where(chosen > 0, jnp.cumsum(chosen, axis=0) - 1, -1)
        recv_pos = lax.all_to_all(pos.T, "ep", 0, 0, tiled=True)
        normed = rms_norm(hidden, norm_w)
        probs = jax.nn.softmax(jnp.dot(normed, router_w, preferred_element_type=jnp.float32), axis=-1)
        y = experts_apply(chips, tp_size, row_limit, normed, recv_pos, w_gate[0], w_up[0], w_down[0])
        out_cols = combine(hidden, pos, probs, y, lax.axis_index("tp"))
        return lax.all_gather(out_cols, "tp", axis=1, tiled=True)

    token_spec = P(("dp", "ep"), None)
    return jax.shard_map(per_device, mesh=mesh, in_specs=(token_spec, token_spec, P(None), P(None, None), P("ep", None, "tp"), P("ep", None, "tp"), P("ep", "tp", None)), out_specs=token_spec, check_vma=False)
```

time: 2260 us -> 613 us (0.27)
  waiting for transfers between devices: 891 us -> 79.2 us
  Pallas kernels: 0 us -> 472 us
  local copies, waits for them, and re-layouts: 459 us -> 15.1 us
  blocking collectives: 377 us -> 0 us
  other arithmetic: 306 us -> 20.6 us
  matrix products: 190 us -> 5.66 us
    psum x1 -> x0, waiting for transfers between devices: 561 us -> none  [per_device(): expert_out = lax.psum(part_out, 'tp')]
    pallas_call x0 -> x2, Pallas kernels: none -> 472 us  [the longest x1 448 us: experts_apply(): pl.pallas_call(functools.partial(expert_kernel, chips, tp_size), out_shap...]
    all_to_all x1 -> x0, blocking collectives: 377 us -> none  [per_device(): lax.all_to_all(send_rows, 'ep', 0, 2, tiled=True)]
    all_to_all x1, waiting for transfers between devices: 330 us -> 0.01 us  [per_device(): recv_pos = lax.all_to_all(pos.T, 'ep', 0, 0, tiled=True)]
    unnamed x3 -> x0, other arithmetic: 196 us -> none
    gather x7 -> x0, local copies, waits for them, and re-layouts: 188 us -> none  [the longest x1 95.7 us: per_device(): back_rows.reshape(n_slots, model_dim)[slot_dest]]
    dot_general x4 -> x1, matrix products: 190 us -> 5.66 us  [per_device(): jnp.dot(normed, router_w, preferred_element_type=jnp.float32)]
    unnamed x21 -> x8, local copies, waits for them, and re-layouts: 145 us -> 9.09 us
  transfers between devices with their start and end apart: 2 -> 2, of which waited for: 2 -> 1; matrix products, arithmetic and copies ran while one was open for 1% -> 4% of each run, Pallas kernels for 0% -> 0%
where the time goes in v1:
time: 613 us; the launch traced here: 612 us
  Pallas kernels  472 us (77%)
  waiting for transfers between devices  79.2 us (13%)
  other arithmetic  20.6 us (3%)
  local copies, waits for them, and re-layouts  15.1 us (2%)
  between operations  13.5 us (2%)
    pallas_call x1, Pallas kernels, experts_apply(): pl.pallas_call(functools.partial(expert_kernel, chips, tp_size), out_shap...  448 us
    all_gather x1, waiting for transfers between devices, per_device(): return lax.all_gather(out_cols, 'tp', axis=1, tiled=True)  79.2 us
    pallas_call x1, Pallas kernels, combine(): pl.pallas_call(combine_kernel, out_shape=jax.ShapeDtypeStruct((toks, widt...  23.4 us
  transfers between devices with their start and end apart: 2, of which 1 were waited for; matrix products, arithmetic and copies ran while one was open for 4% of the time, Pallas kernels for 0%

profile of v1, /device:TPU:97, one launch (start us, length us, event | category | flops | bytes accessed | tf_op | source)
XLA Modules:
  0.0 611.9 jit_solution(14167962128076841537)
XLA Ops:
  6.5 0.0 copy-start
  6.6 0.0 copy-start.2
  6.6 0.8 convert_reduce_fusion
  7.3 0.3 copy.30
  7.6 0.3 copy.31
  7.9 2.3 reduce-window.6
  10.2 0.3 slice_reduce_fusion
  10.5 0.2 reduce-window.9
  10.7 0.1 add_add_fusion
  10.8 0.3 copy.32
  11.1 0.1 bitcast_select_fusion.1
  11.3 0.9 copy.36
  12.2 6.0 all-to-all-start
  18.2 0.0 all-gather.2.cloned.1.call-start
  18.2 5.1 fusion
  23.3 0.0 copy-done.2
  23.3 8.7 %fusion.2.v_ref = bf16[2048,2048]{1,0:T(8,128)(2,1)} fusion(bf16[2048,2048]{1,0:T(8,128)(2,1)} %param.7, f32[2048]{0:T(1024)S(1)} %convert_element_type.14, f32[2048]{0:T(1024)S(1)} %add_rsqrt_fusion), kind=kLoop, calls=%fused_computation.4 | loop fusion | flops 16777216 | bytes 16793600 | tf_op jit(solution)/shard_map/convert_element_type | solution.py:22
  32.1 0.0 copy-done
  32.1 5.7 fusion.5
  37.7 0.3 copy.34
  38.1 0.7 fusion.4
  38.7 1.5 fusion.3.prob_ref
  40.3 0.4 copy.33
  40.7 1.1 bitcast_select_fusion.pos_ref
  41.8 3.1 constant_dynamic-slice_fusion.hidden_ref
  44.9 0.0 all-to-all-done
  44.9 0.6 copy.39
  45.5 448.3 %experts.1 = (bf16[7,2048,2048]{2,1,0:T(8,128)(2,1)}, bf16[8,1024,512]{2,1,0:T(8,128)(2,1)}) custom-call(bf16[2048,2048]{1,0:T(8,128)(2,1)} %fusion.2.v_ref, s32[8,2048]{1,0:T(8,128)} %bitcast.23, bf16[2048,1408]{1,0:T(8,128)(2,1)} %bitcast.25, bf16[2048,1408]{1,0:T(8,128)(2,1)} %bitcast.26, bf16[1408,2048]{1,0:T(8,128)(2,1)} %bitcast.27), custom_call_target="tpu_custom_call" | custom-call | flops 210453397504 | bytes 84410368 | tf_op jit(solution)/shard_map/experts/pallas_call | solution.py:257
  493.9 23.4 %combine.1 = bf16[2048,512]{1,0:T(8,128)(2,1)} custom-call(bf16[2048,512]{1,0:T(8,128)(2,1)} %constant_dynamic-slice_fusion.hidden_ref, s32[2048,8]{1,0:T(8,128)} %bitcast_select_fusion.pos_ref, f32[2048,8]{1,0:T(8,128)} %fusion.3.prob_ref, bf16[8,1024,512]{2,1,0:T(8,128)(2,1)} %get-tuple-element.6.y_ref), custom_call_target="tpu_custom_call" | custom-call | flops 17179869184 | bytes 16777216 | tf_op jit(solution)/shard_map/combine/pallas_call | solution.py:289
  517.3 0.1 all-gather.2.cloned.1.call-update
  517.4 0.0 copy-start.1
  517.4 79.2 %all-gather.2.cloned.1.call-done = bf16[2048,2048]{1,0:T(8,128)(2,1)} async-done(((bf16[2048,512]{1,0:T(8,128)(2,1)}), bf16[2048,2048]{1,0:T(8,128)(2,1)}) %all-gather.2.cloned.1.call-update) | async-done | bytes 8388624 | tf_op jit(solution)/shard_map/all_gather | solution.py:319
  596.6 8.4 %copy.41 = bf16[2048,2048]{1,0:T(8,128)(2,1)} copy(bf16[2048,2048]{1,0:T(8,128)(2,1)} %all-gather.2.cloned.1.call-done) | data formatting | bytes 16777216
  605.0 0.0 copy-done.1
  (3 shorter events, 0.0 us)
Async XLA Ops:
  6.5 25.5 %copy-start = (bf16[2048,8]{0,1:T(8,128)(2,1)S(1)}, bf16[2048,8]{0,1:T(8,128)(2,1)}, u32[]{:S(2)}) copy-start(bf16[2048,8]{0,1:T(8,128)(2,1)} %param.10) | copy-start | bytes 98308
  6.6 16.8 %copy-start.2 = (bf16[2048]{0:T(1024)(128)(2,1)S(1)}, bf16[2048]{0:T(1024)(128)(2,1)}, u32[]{:S(2)}) copy-start(bf16[2048]{0:T(1024)(128)(2,1)} %param.9) | copy-start | bytes 12292
  12.2 32.7 %all-to-all-start = ((s32[8,1,2048]{2,1,0:T(1,128)}), s32[8,1,2048]{2,1,0:T(1,128)S(1)}, u32[]{:S(2)}, u32[]{:S(2)}) async-start(s32[8,1,2048]{2,1,0:T(1,128)} %copy.36), calls=%async_computation | async-start | bytes 131072 | tf_op jit(solution)/shard_map/all_to_all | solution.py:314
  18.2 578.4 %all-gather.2.cloned.1.call-start = ((), (), s32[]{:S(2)}) async-start(), calls=%async_computation.1 | async-start | bytes 10485760 | tf_op jit(solution)/shard_map/all_gather | solution.py:319
  517.4 87.6 %copy-start.1 = (bf16[2048,8]{0,1:T(8,128)(2,1)S(1)}, bf16[2048,8]{0,1:T(8,128)(2,1)}, u32[]{:S(2)}) copy-start(bf16[2048,8]{0,1:T(8,128)(2,1)} %param.10) | copy-start | bytes 98308
Sparse Core Ops, SparseCore 0:
  517.5 79.0 all-gather.1

commit v2 on v1

v2 whole, which is shorter than its diff:
```python
import functools

import jax
import jax.numpy as jnp
from jax import lax
from jax.experimental import pallas as pl
from jax.experimental.pallas import tpu as pltpu
from jax.sharding import PartitionSpec as P

NORM_EPS = 1e-6
VMEM_LIMIT = 60 * 1024 * 1024
SLOT_TILE = 256
RING = 4
MESH = pl.DeviceIdType.MESH
BLOCKS = ((0, 0), (0, 1), (-1, 0), (1, 0), (-1, 1), (1, 1), (2, 0), (2, 1))


def rms_norm(hidden, norm_w):
    wide_h = hidden.astype(jnp.float32)
    mean_sq = jnp.mean(wide_h * wide_h, axis=-1, keepdims=True)
    return (wide_h * lax.rsqrt(mean_sq + NORM_EPS) * norm_w.astype(jnp.float32)).astype(jnp.bfloat16)


def row_cap(tok_dev, top_k, n_experts):
    return 8 * ((2 * top_k * tok_dev + 8 * n_experts - 1) // (8 * n_experts))


def norm_kernel(hidden_ref, w_ref, out_ref):
    out_ref[...] = rms_norm(hidden_ref[...], w_ref[...])


def norm_rows(hidden, norm_w):
    toks, dim = hidden.shape
    tile = pl.BlockSpec((SLOT_TILE, dim), lambda i: (i, 0))
    return pl.pallas_call(
        norm_kernel,
        out_shape=jax.ShapeDtypeStruct((toks, dim), jnp.bfloat16),
        grid=(toks // SLOT_TILE,),
        in_specs=[tile, pl.BlockSpec((1, dim), lambda i: (0, 0))],
        out_specs=tile,
        cost_estimate=pl.CostEstimate(flops=6 * toks * dim, bytes_accessed=4 * toks * dim, transcendentals=toks),
        name="norm_rows",
    )(hidden, norm_w.reshape(1, dim))


def remote(src, dst, send, recv, device):
    return pltpu.make_async_remote_copy(src_ref=src, dst_ref=dst, send_sem=send, recv_sem=recv, device_id=device, device_id_type=MESH)


def enter(peers):
    barrier = pltpu.get_barrier_semaphore()
    for peer in peers:
        pl.semaphore_signal(barrier, inc=1, device_id=peer, device_id_type=MESH)
    pl.semaphore_wait(barrier, len(peers))


def expert_kernel(chips, tp_size, v_ref, pos_ref, gate_hbm, up_hbm, down_hbm, vbuf, home,
                  gate_ref, up_ref, down_ref, v_now, pos_now, stage, recv_f, recv_c, recv_d, fin,
                  w_sem, v_sem, part_sem, hop_send, hop_recv, pair_send, pair_recv, fwd_send, fwd_recv,
                  near_send, near_recv, far_send, far_recv,
                  f_send, f_recv, c_send, c_recv, d_send, d_recv, home_send, home_recv, own_sem):
    y = lax.axis_index("tp")
    me = lax.axis_index("ep")
    chip, core = me // 2, me % 2
    row_part, dim = v_ref.shape[2:]
    tok_dev = 2 * tp_size * row_part
    short = row_part // 2
    n_tiles = home.shape[1] // SLOT_TILE
    steps = len(BLOCKS) * n_tiles
    wide = dim // tp_size
    side = wide // 2
    to_ep = lambda dx, c: {"ep": 2 * lax.rem(chip + dx + chips, chips) + c}
    to_tp = lambda dy: {"tp": lax.rem(y + dy + tp_size, tp_size)}
    partner = to_ep(0, 1 - core)

    weights = [pltpu.make_async_copy(a, b, w_sem.at[j]) for j, (a, b) in enumerate(((gate_hbm, gate_ref), (up_hbm, up_ref), (down_hbm, down_ref)))]
    for w in weights:
        w.start()
    enter([to_tp(1), to_tp(-1), partner] + [to_ep(dx, c) for dx in (-1, 1, 2) for c in (0, 1)])

    at = lambda dx, sc: BLOCKS.index((dx, sc)) - 1
    way = lambda sign: (sign + 1) // 2

    def swap(j):
        c = 1 - core if j == 0 else core
        return remote(v_ref.at[:, c], vbuf.at[0, :, c], part_sem.at[0, j], part_sem.at[1, j], partner)

    def swap_arrival(j):
        c = core if j == 0 else 1 - core
        return remote(v_ref.at[:, c], vbuf.at[0, :, c], part_sem.at[0, j], part_sem.at[1, j], partner)

    def hop(sc, sign, own):
        src = v_ref if own else vbuf.at[0]
        part = slice(None) if sc == 0 else y
        return remote(src.at[part, core], vbuf.at[at(-sign, sc), part, core], hop_send.at[sc, way(sign)], hop_recv.at[sc, way(sign)], to_ep(sign, core))

    def near(sign, d, q):
        part = vbuf.at[at(sign, 1), q, core]
        return remote(part, part, near_send.at[way(sign), d], near_recv.at[way(sign), d], to_tp(1 - 2 * d))

    def far(sign, d, q):
        part = vbuf.at[at(sign, 1), q, core, pl.ds(d * short, short)]
        return remote(part, part, far_send.at[way(sign), d], far_recv.at[way(sign), d], to_tp(1 - 2 * d))

    def forward(sc, sign):
        rows = pl.ds(way(-sign) * short, short)
        return remote(vbuf.at[at(-sign, sc), :, core, rows], vbuf.at[at(2, sc), :, core, rows], fwd_send.at[sc, way(sign)], fwd_recv.at[sc, way(sign)], to_ep(sign, core))

    def pair(k):
        return remote(vbuf.at[k - 1, :, core], vbuf.at[k - 1, :, core], pair_send.at[k], pair_recv.at[k], partner)

    def pair_arrival(k):
        return remote(vbuf.at[k - 1, :, 1 - core], vbuf.at[k - 1, :, 1 - core], pair_send.at[k], pair_recv.at[k], partner)

    around = lambda dy: lax.rem(y + dy + tp_size, tp_size)

    swap(0).start()
    swap(1).start()

    @pl.when(core == 0)
    def _():
        swap_arrival(0).wait_recv()
        for sc in (1, 0):
            for sign in (1, -1):
                hop(sc, sign, sc == 0).start()

    @pl.when(core == 1)
    def _():
        for sign in (1, -1):
            hop(1, sign, True).start()
        swap_arrival(0).wait_recv()
        for sign in (1, -1):
            hop(0, sign, False).start()

    def load(src, row):
        copy = pltpu.make_async_copy(src, v_now, v_sem)
        copy.start()
        pos_now[...] = pos_ref[pl.ds(row, 1), :]
        copy.wait()

    def spread():
        for sign in (1, -1):
            hop(1, sign, True).wait_recv()
            for d in (0, 1):
                near(-sign, d, y).start()

    def block_start(k):
        dx, sc = BLOCKS[k]
        if k == 0:
            for w in weights:
                w.wait()
            load(v_ref, me)
            return
        if k == 1:
            swap_arrival(1).wait_recv()
            load(vbuf.at[0], 2 * chip + 1 - core)
            return
        if k == 2:
            for sign in (-1, 1):
                for d in (0, 1):
                    q = around(2 * d - 1)
                    near(sign, d, q).wait_recv()
                    far(sign, d, q).start()
            for sign in (1, -1):
                hop(0, sign, True).wait_recv()
                forward(0, sign).start()
                pair(BLOCKS.index((-sign, 0))).start()
        if k == 3:
            for sign in (1, -1):
                for d in (0, 1):
                    far(-sign, d, around(2)).wait_recv()
                forward(1, sign).start()
                pair(BLOCKS.index((-sign, 1))).start()
        if k in (5, 6):
            for sign in (1, -1):
                forward(k - 5, sign).wait_recv()
            pair(k + 1).start()
        pair_arrival(k).wait_recv()
        load(vbuf.at[k - 1], 2 * lax.rem(chip + dx + chips, chips) + sc)

    def f_copy(s, d):
        return remote(stage.at[s, 3, d], recv_f.at[d, s], f_send.at[d, s], f_recv.at[d, s], to_tp(1 - 2 * d))

    def c_copy(s, d):
        return remote(stage.at[s, 1 + d, d], recv_c.at[d, s], c_send.at[d, s], c_recv.at[d, s], to_tp(1 - 2 * d))

    def d_copy(s, d):
        return remote(stage.at[s, 1 + d, 1 - d], recv_d.at[d, s], d_send.at[d, s], d_recv.at[d, s], to_tp(1 - 2 * d))

    def rows_of(tile):
        return pl.ds(pl.multiple_of(tile * SLOT_TILE, SLOT_TILE), SLOT_TILE)

    def home_copy(k, s, tile):
        dx, sc = BLOCKS[k]
        device = partner if k == 1 else to_ep(dx, sc)
        return remote(fin.at[s], home.at[me, rows_of(tile)], home_send.at[s], home_recv, device)

    def own_copy(s, tile):
        return pltpu.make_async_copy(fin.at[s], home.at[me, rows_of(tile)], own_sem.at[s])

    def step(i, carry):
        @pl.when(i == n_tiles - 1)
        def _():
            spread()

        for k in range(len(BLOCKS)):
            @pl.when(i == k * n_tiles)
            def _(k=k):
                block_start(k)

        @pl.when(i < steps)
        def _():
            s = lax.rem(i, RING)

            @pl.when(i >= RING)
            def _():
                for d in (0, 1):
                    f_copy(s, d).wait_send()
                    c_copy(s, d).wait_send()
                    d_copy(s, d).wait_send()

            slots = lax.rem(i, n_tiles) * SLOT_TILE + lax.broadcasted_iota(jnp.int32, (SLOT_TILE, tok_dev), 0)
            pick = jnp.where(pos_now[...] == slots, 1.0, 0.0).astype(jnp.bfloat16)
            rows = jnp.dot(pick, v_now[...].reshape(tok_dev, dim), preferred_element_type=jnp.float32).astype(jnp.bfloat16)
            gate_pre = jnp.dot(rows, gate_ref[...], preferred_element_type=jnp.float32)
            up_pre = jnp.dot(rows, up_ref[...], preferred_element_type=jnp.float32)
            act = (jax.nn.silu(gate_pre) * up_pre).astype(jnp.bfloat16)
            for part, dy in ((3, 2), (1, 1), (2, -1), (0, 0)):
                q = lax.rem(y + dy + tp_size, tp_size)
                for d in (0, 1):
                    cols = pl.ds(pl.multiple_of(q * wide + d * side, side), side)
                    stage[s, part, d] = jnp.dot(act, down_ref[:, cols], preferred_element_type=jnp.float32).astype(jnp.bfloat16)
            for d in (0, 1):
                f_copy(s, d).start()
            for d in (0, 1):
                d_copy(s, d).start()

        @pl.when(i >= 2)
        def _():
            j = i - 2
            s = lax.rem(j, RING)
            tile = lax.rem(j, n_tiles)
            for d in (0, 1):
                c_copy(s, d).wait_recv()
                d_copy(s, d).wait_recv()

            @pl.when((j >= RING) & (j < RING + n_tiles))
            def _():
                own_copy(s, tile).wait()

            @pl.when(j >= RING + n_tiles)
            def _():
                home_copy(2, s, tile).wait_send()

            f32 = lambda a: a.astype(jnp.float32)
            for d in (0, 1):
                total = f32(stage[s, 0, d]) + f32(recv_c[d, s]) + f32(recv_d[1 - d, s])
                fin[s, :, d * side:(d + 1) * side] = total.astype(jnp.bfloat16)

            @pl.when(j < n_tiles)
            def _():
                own_copy(s, tile).start()

            for k in range(1, len(BLOCKS)):
                @pl.when(j // n_tiles == k)
                def _(k=k):
                    home_copy(k, s, tile).start()

        @pl.when((i >= 1) & (i <= steps))
        def _():
            s = lax.rem(i - 1, RING)
            for d in (0, 1):
                f_copy(s, d).wait_recv()
                stage[s, 1 + d, d] = (stage[s, 1 + d, d].astype(jnp.float32) + recv_f[d, s].astype(jnp.float32)).astype(jnp.bfloat16)
                c_copy(s, d).start()

        return carry

    assert n_tiles == RING
    lax.fori_loop(0, steps + 2, step, 0)

    for s in range(RING):
        for d in (0, 1):
            f_copy(s, d).wait_send()
            c_copy(s, d).wait_send()
            d_copy(s, d).wait_send()
        home_copy(2, s, s).wait_send()
    for j in (0, 1):
        swap(j).wait_send()
    for sc in (0, 1):
        for sign in (1, -1):
            hop(sc, sign, True).wait_send()
            forward(sc, sign).wait_send()
    for sign in (1, -1):
        for d in (0, 1):
            near(sign, d, y).wait_send()
            far(sign, d, y).wait_send()
    for k in range(2, len(BLOCKS)):
        pair(k).wait_send()
    arrived = home.at[pl.ds(0, home.shape[0] - 1)]
    remote(arrived, arrived, home_send.at[0], home_recv, partner).wait_recv()


def experts_apply(chips, tp_size, row_limit, v, pos_rows, gate, up, down):
    tok_dev, dim = v.shape
    ff = gate.shape[1]
    width = dim // tp_size
    side = width // 2
    n = len(BLOCKS)
    bf16 = jnp.bfloat16
    anywhere = pl.BlockSpec(memory_space=pl.ANY)
    dma = pltpu.SemaphoreType.DMA
    ring = (2, RING, SLOT_TILE, side)
    parts = (tp_size, 2, tok_dev // (2 * tp_size), dim)
    return pl.pallas_call(
        functools.partial(expert_kernel, chips, tp_size),
        out_shape=(jax.ShapeDtypeStruct((n - 1, *parts), bf16), jax.ShapeDtypeStruct((n, row_limit, width), bf16)),
        in_specs=[anywhere, pl.BlockSpec(memory_space=pltpu.VMEM), anywhere, anywhere, anywhere],
        out_specs=(anywhere, anywhere),
        scratch_shapes=[
            pltpu.VMEM((dim, ff), bf16), pltpu.VMEM((dim, ff), bf16), pltpu.VMEM((ff, dim), bf16),
            pltpu.VMEM(parts, bf16), pltpu.VMEM((1, tok_dev), jnp.int32),
            pltpu.VMEM((RING, 4, 2, SLOT_TILE, side), bf16), pltpu.VMEM(ring, bf16), pltpu.VMEM(ring, bf16), pltpu.VMEM(ring, bf16),
            pltpu.VMEM((RING, SLOT_TILE, width), bf16),
            dma((3,)), dma, dma((2, 2)), dma((2, 2)), dma((2, 2)), dma((n,)), dma((n,)), dma((2, 2)), dma((2, 2)),
            dma((2, 2)), dma((2, 2)), dma((2, 2)), dma((2, 2)),
            dma((2, RING)), dma((2, RING)), dma((2, RING)), dma((2, RING)), dma((2, RING)), dma((2, RING)),
            dma((RING,)), dma, dma((RING,)),
        ],
        cost_estimate=pl.CostEstimate(flops=2 * n * row_limit * dim * (tok_dev + 3 * ff), bytes_accessed=2 * (n * tok_dev * dim + 3 * dim * ff), transcendentals=n * row_limit * ff),
        compiler_params=pltpu.CompilerParams(collective_id=0, has_side_effects=True, vmem_limit_bytes=VMEM_LIMIT),
        name="experts",
    )(v.reshape(parts), pos_rows, gate, up, down)[1]


def finish_kernel(tp_size, pos_ref, router_ref, y_ref, hidden_hbm, v_hbm, out, hidden_ref, v_ref, done, v_sem, hidden_sem, own_sem, near_send, near_recv, far_send, far_recv):
    y = lax.axis_index("tp")
    width = done.shape[1]
    tiles = done.shape[0] // SLOT_TILE
    short = SLOT_TILE // 2
    to_tp = lambda dy: {"tp": lax.rem(y + dy + tp_size, tp_size)}
    cols = lambda dy: pl.ds(pl.multiple_of(lax.rem(y + dy + tp_size, tp_size) * width, width), width)
    rows_of = lambda t: pl.ds(pl.multiple_of(t * SLOT_TILE, SLOT_TILE), SLOT_TILE)

    fetch_v = lambda t: pltpu.make_async_copy(v_hbm.at[rows_of(t)], v_ref.at[rows_of(t)], v_sem.at[t])
    fetch_h = pltpu.make_async_copy(hidden_hbm.at[:, cols(0)], hidden_ref, hidden_sem)
    fetch_h.start()
    for t in range(tiles):
        fetch_v(t).start()
    enter([to_tp(1), to_tp(-1)])

    own = lambda t: pltpu.make_async_copy(done.at[rows_of(t)], out.at[rows_of(t), cols(0)], own_sem.at[t])

    def near(t, d, dy):
        return remote(done.at[rows_of(t)], out.at[rows_of(t), cols(dy)], near_send.at[d, t], near_recv.at[d, t], to_tp(1 - 2 * d))

    def far(t, d, dy):
        part = out.at[pl.ds(pl.multiple_of(t * SLOT_TILE + d * short, short), short), cols(dy)]
        return remote(part, part, far_send.at[d, t], far_recv.at[d, t], to_tp(1 - 2 * d))

    fetch_h.wait()

    def step(t, carry):
        @pl.when(t < tiles)
        def _():
            fetch_v(t).wait()
            rows = rows_of(t)
            logits = jnp.dot(v_ref[rows, :], router_ref[...], preferred_element_type=jnp.float32)
            probs = jax.nn.softmax(logits, axis=-1)
            acc = hidden_ref[rows, :].astype(jnp.float32)
            pos = pos_ref[rows, :]
            for e in range(y_ref.shape[0]):
                slots = lax.broadcasted_iota(jnp.int32, (SLOT_TILE, y_ref.shape[1]), 1)
                pick = jnp.where(pos[:, e:e + 1] == slots, 1.0, 0.0).astype(jnp.bfloat16)
                acc += probs[:, e:e + 1] * jnp.dot(pick, y_ref[e], preferred_element_type=jnp.float32)
            done[rows, :] = acc.astype(done.dtype)
            own(t).start()
            for d in (0, 1):
                near(t, d, 0).start()

        @pl.when(t >= 1)
        def _():
            for d in (0, 1):
                near(t - 1, d, 2 * d - 1).wait_recv()
                far(t - 1, d, 2 * d - 1).start()

        return carry

    lax.fori_loop(0, tiles + 1, step, 0)
    for t in range(tiles):
        own(t).wait()
        for d in (0, 1):
            near(t, d, 0).wait_send()
            far(t, d, 2 * d - 1).wait_send()
            far(t, d, 2).wait_recv()


def finish(tp_size, hidden, v, pos, router_w, y):
    toks, dim = hidden.shape
    n, limit, width = y.shape
    tiles = toks // SLOT_TILE
    anywhere = pl.BlockSpec(memory_space=pl.ANY)
    vmem = pl.BlockSpec(memory_space=pltpu.VMEM)
    dma = pltpu.SemaphoreType.DMA
    return pl.pallas_call(
        functools.partial(finish_kernel, tp_size),
        out_shape=jax.ShapeDtypeStruct((toks, dim), hidden.dtype),
        in_specs=[vmem, vmem, vmem, anywhere, anywhere],
        out_specs=anywhere,
        scratch_shapes=[pltpu.VMEM((toks, width), hidden.dtype), pltpu.VMEM((toks, dim), v.dtype), pltpu.VMEM((toks, width), hidden.dtype),
                        dma((tiles,)), dma, dma((tiles,)), dma((2, tiles)), dma((2, tiles)), dma((2, tiles)), dma((2, tiles))],
        cost_estimate=pl.CostEstimate(flops=2 * toks * limit * width * n, bytes_accessed=2 * n * limit * width + 8 * toks * width, transcendentals=0),
        compiler_params=pltpu.CompilerParams(collective_id=1, has_side_effects=True, vmem_limit_bytes=VMEM_LIMIT),
        name="finish",
    )(pos, router_w, y, hidden, v)


def solution(mesh):
    chips = mesh.shape["ep"] // 2
    tp_size = mesh.shape["tp"]

    def per_device(hidden, expert_ids, norm_w, router_w, w_gate, w_up, w_down):
        tok_dev = hidden.shape[0]
        top_k = expert_ids.shape[1]
        n_experts = router_w.shape[1]
        row_limit = row_cap(tok_dev, top_k, n_experts)
        experts = jnp.arange(n_experts, dtype=jnp.int32)
        chosen = jnp.sum((expert_ids[:, :, None] == experts).astype(jnp.int32), axis=1)
        pos = jnp.where(chosen > 0, jnp.cumsum(chosen, axis=0) - 1, -1)
        recv_pos = lax.all_to_all(pos.T, "ep", 0, 0, tiled=True)
        normed = norm_rows(hidden, norm_w)
        y = experts_apply(chips, tp_size, row_limit, normed, recv_pos, w_gate[0], w_up[0], w_down[0])
        return finish(tp_size, hidden, normed, pos, router_w, y)

    token_spec = P(("dp", "ep"), None)
    return jax.shard_map(per_device, mesh=mesh, in_specs=(token_spec, token_spec, P(None), P(None, None), P("ep", None, "tp"), P("ep", None, "tp"), P("ep", "tp", None)), out_specs=token_spec, check_vma=False)
```

time: 613 us -> 521 us (0.85)
  waiting for transfers between devices: 79.2 us -> 0.01 us
  Pallas kernels: 472 us -> 497 us
  other arithmetic: 20.6 us -> 4.51 us
  between operations: 13.5 us -> 0.07 us
    all_gather x1 -> x0, waiting for transfers between devices: 79.2 us -> none  [per_device(): return lax.all_gather(out_cols, 'tp', axis=1, tiled=True)]
    pallas_call x1 -> x2, Pallas kernels: 23.4 us -> 88.9 us  [the longest x1 78.7 us: finish(): pl.pallas_call(functools.partial(finish_kernel, tp_size), out_shape=jax.S...]
    pallas_call x1, Pallas kernels: 448 us -> 408 us  [experts_apply(): pl.pallas_call(functools.partial(expert_kernel, chips, tp_size), out_shap...]
    convert_element_type x2 -> x0, other arithmetic: 8.74 us -> none  [the longest x1 8.74 us: rms_norm(): (wide_h * lax.rsqrt(mean_sq + NORM_EPS) * norm_w.astype(jnp.float32)).ast...]
  transfers between devices with their start and end apart: 2 -> 1, of which waited for: 1 -> 0; matrix products, arithmetic and copies ran while one was open for 4% -> 1% of each run, Pallas kernels for 0% -> 2%
where the time goes in v2:
time: 521 us
  Pallas kernels  497 us (95%)
  local copies, waits for them, and re-layouts  13.3 us (3%)
  starting transfers between devices  6.01 us (1%)
    pallas_call x1, Pallas kernels, experts_apply(): pl.pallas_call(functools.partial(expert_kernel, chips, tp_size), out_shap...  408 us
    pallas_call x1, Pallas kernels, finish(): pl.pallas_call(functools.partial(finish_kernel, tp_size), out_shape=jax.S...  78.7 us
  transfers between devices with their start and end apart: 1, of which 0 were waited for; matrix products, arithmetic and copies ran while one was open for 1% of the time, Pallas kernels for 2%

profile of v2, /device:TPU:97, one launch (start us, length us, event | category | flops | bytes accessed | tf_op | source)
XLA Modules:
  0.0 520.6 jit_solution(9917080875764461885)
XLA Ops:
  0.0 0.0 copy-start.1
  0.0 0.0 copy-start
  0.0 0.8 convert_reduce_fusion
  0.8 0.3 copy.30
  1.1 0.3 copy.31
  1.4 2.3 reduce-window.6
  3.7 0.3 slice_reduce_fusion
  4.0 0.2 reduce-window.9
  4.2 0.1 add_add_fusion
  4.2 0.3 copy.32
  4.6 0.1 bitcast_select_fusion.1
  4.7 0.9 copy.34
  5.6 6.0 %all-to-all-start = ((s32[8,1,2048]{2,1,0:T(1,128)}), s32[8,1,2048]{2,1,0:T(1,128)S(1)}, u32[]{:S(2)}, u32[]{:S(2)}) async-start(s32[8,1,2048]{2,1,0:T(1,128)} %copy.34), calls=%async_computation | async-start | bytes 131072 | tf_op jit(solution)/shard_map/all_to_all | solution.py:430
  11.7 0.4 copy.33
  12.1 1.1 bitcast_select_fusion.pos_ref
  13.2 0.0 copy-done.1
  13.2 0.6 reshape.25.w_ref
  13.8 0.0 copy-done
  13.8 1.0 copy.35.router_ref
  14.8 10.2 %norm_rows.1.v_hbm = bf16[2048,2048]{1,0:T(8,128)(2,1)} custom-call(bf16[2048,2048]{1,0:T(8,128)(2,1)} %hidden_hbm.1, bf16[1,2048]{1,0:T(2,128)(2,1)} %reshape.25.w_ref), custom_call_target="tpu_custom_call" | custom-call | flops 25165824 | bytes 16777216 | tf_op jit(solution)/shard_map/norm_rows/pallas_call | solution.py:35
  25.0 0.0 all-to-all-done
  25.0 0.6 copy.38
  25.7 407.8 %experts.1 = (bf16[7,4,2,256,2048]{4,3,2,1,0:T(8,128)(2,1)}, bf16[8,1024,512]{2,1,0:T(8,128)(2,1)}) custom-call(bf16[4,2,256,2048]{3,2,1,0:T(8,128)(2,1)} %bitcast.21, s32[8,2048]{1,0:T(8,128)} %bitcast.23, bf16[2048,1408]{1,0:T(8,128)(2,1)} %bitcast.25, bf16[2048,1408]{1,0:T(8,128)(2,1)} %bitcast.26, bf16[1408,2048]{1,0:T(8,128)(2,1)} %bitcast.27), custom_call_target="tpu_custom_call" | custom-call | flops 210453397504 | bytes 84410368 | tf_op jit(solution)/shard_map/experts/pallas_call | solution.py:315
  433.5 78.7 %finish.1 = bf16[2048,2048]{1,0:T(8,128)(2,1)} custom-call(s32[2048,8]{1,0:T(8,128)} %bitcast_select_fusion.pos_ref, bf16[2048,8]{1,0:T(8,128)(2,1)} %copy.35.router_ref, bf16[8,1024,512]{2,1,0:T(8,128)(2,1)} %get-tuple-element.6.y_ref, bf16[2048,2048]{1,0:T(8,128)(2,1)} %hidden_hbm.1, bf16[2048,2048]{1,0:T(8,128)(2,1)} %norm_rows.1.v_hbm), custom_call_target="tpu_custom_call" | custom-call | flops 17179869184 | bytes 16777216 | tf_op jit(solution)/shard_map/finish/pallas_call | solution.py:405
  512.2 8.4 %copy.40 = bf16[2048,2048]{1,0:T(8,128)(2,1)} copy(bf16[2048,2048]{1,0:T(8,128)(2,1)} %finish.1) | data formatting | bytes 16777216
  (1 shorter events, 0.0 us)
Async XLA Ops:
  0.0 13.2 %copy-start.1 = (bf16[2048]{0:T(1024)(128)(2,1)S(1)}, bf16[2048]{0:T(1024)(128)(2,1)}, u32[]{:S(2)}) copy-start(bf16[2048]{0:T(1024)(128)(2,1)} %param.9) | copy-start | bytes 12292
  0.0 13.8 %copy-start = (bf16[2048,8]{0,1:T(8,128)(2,1)S(1)}, bf16[2048,8]{0,1:T(8,128)(2,1)}, u32[]{:S(2)}) copy-start(bf16[2048,8]{0,1:T(8,128)(2,1)} %param.10) | copy-start | bytes 98308
  5.6 19.4 %all-to-all-start = ((s32[8,1,2048]{2,1,0:T(1,128)}), s32[8,1,2048]{2,1,0:T(1,128)S(1)}, u32[]{:S(2)}, u32[]{:S(2)}) async-start(s32[8,1,2048]{2,1,0:T(1,128)} %copy.34), calls=%async_computation | async-start | bytes 131072 | tf_op jit(solution)/shard_map/all_to_all | solution.py:430

commit v3 on v2

--- a/solution.py
+++ b/solution.py
@@ -8,9 +8,13 @@
 from jax.sharding import PartitionSpec as P
 
 NORM_EPS = 1e-6
-VMEM_LIMIT = 60 * 1024 * 1024
+VMEM_LIMIT = 63 * 1024 * 1024
 SLOT_TILE = 256
-RING = 4
+NORM_TILE = 512
+RING = 8
+FIN = 4
+CHAIN = 2
+FINAL = 4
 MESH = pl.DeviceIdType.MESH
 BLOCKS = ((0, 0), (0, 1), (-1, 0), (1, 0), (-1, 1), (1, 1), (2, 0), (2, 1))
 
@@ -31,11 +35,11 @@
 
 def norm_rows(hidden, norm_w):
     toks, dim = hidden.shape
-    tile = pl.BlockSpec((SLOT_TILE, dim), lambda i: (i, 0))
+    tile = pl.BlockSpec((NORM_TILE, dim), lambda i: (i, 0))
     return pl.pallas_call(
         norm_kernel,
         out_shape=jax.ShapeDtypeStruct((toks, dim), jnp.bfloat16),
-        grid=(toks // SLOT_TILE,),
+        grid=(toks // NORM_TILE,),
         in_specs=[tile, pl.BlockSpec((1, dim), lambda i: (0, 0))],
         out_specs=tile,
         cost_estimate=pl.CostEstimate(flops=6 * toks * dim, bytes_accessed=4 * toks * dim, transcendentals=toks),
@@ -132,11 +136,19 @@
         for sign in (1, -1):
             hop(0, sign, False).start()
 
-    def load(src, row):
-        copy = pltpu.make_async_copy(src, v_now, v_sem)
-        copy.start()
-        pos_now[...] = pos_ref[pl.ds(row, 1), :]
-        copy.wait()
+    def load(k):
+        src = v_ref if k == 0 else vbuf.at[k - 1]
+        return pltpu.make_async_copy(src, v_now.at[k % 2], v_sem.at[k % 2])
+
+    def fetch(k):
+        dx, sc = BLOCKS[k]
+        if k == 1:
+            swap_arrival(1).wait_recv()
+        if k > 1:
+            pair_arrival(k).wait_recv()
+        load(k).start()
+        row = (me, 2 * chip + 1 - core)[k] if k < 2 else 2 * lax.rem(chip + dx + chips, chips) + sc
+        pos_now[k % 2] = pos_ref[pl.ds(row, 1), :]
 
     def spread():
         for sign in (1, -1):
@@ -145,16 +157,10 @@
                 near(-sign, d, y).start()
 
     def block_start(k):
-        dx, sc = BLOCKS[k]
         if k == 0:
+            fetch(0)
             for w in weights:
                 w.wait()
-            load(v_ref, me)
-            return
-        if k == 1:
-            swap_arrival(1).wait_recv()
-            load(vbuf.at[0], 2 * chip + 1 - core)
-            return
         if k == 2:
             for sign in (-1, 1):
                 for d in (0, 1):
@@ -165,6 +171,7 @@
                 hop(0, sign, True).wait_recv()
                 forward(0, sign).start()
                 pair(BLOCKS.index((-sign, 0))).start()
+            fetch(2)
         if k == 3:
             for sign in (1, -1):
                 for d in (0, 1):
@@ -175,8 +182,7 @@
             for sign in (1, -1):
                 forward(k - 5, sign).wait_recv()
             pair(k + 1).start()
-        pair_arrival(k).wait_recv()
-        load(vbuf.at[k - 1], 2 * lax.rem(chip + dx + chips, chips) + sc)
+        load(k).wait()
 
     def f_copy(s, d):
         return remote(stage.at[s, 3, d], recv_f.at[d, s], f_send.at[d, s], f_recv.at[d, s], to_tp(1 - 2 * d))
@@ -199,6 +205,12 @@
         return pltpu.make_async_copy(fin.at[s], home.at[me, rows_of(tile)], own_sem.at[s])
 
     def step(i, carry):
+        for k in range(1, len(BLOCKS)):
+            if k != 2:
+                @pl.when(i == k * n_tiles - 1)
+                def _(k=k):
+                    fetch(k)
+
         @pl.when(i == n_tiles - 1)
         def _():
             spread()
@@ -219,56 +231,59 @@
                     c_copy(s, d).wait_send()
                     d_copy(s, d).wait_send()
 
+            now = lax.rem(i // n_tiles, 2)
             slots = lax.rem(i, n_tiles) * SLOT_TILE + lax.broadcasted_iota(jnp.int32, (SLOT_TILE, tok_dev), 0)
-            pick = jnp.where(pos_now[...] == slots, 1.0, 0.0).astype(jnp.bfloat16)
-            rows = jnp.dot(pick, v_now[...].reshape(tok_dev, dim), preferred_element_type=jnp.float32).astype(jnp.bfloat16)
+            pick = jnp.where(pos_now[now] == slots, 1.0, 0.0).astype(jnp.bfloat16)
+            rows = jnp.dot(pick, v_now[now].reshape(tok_dev, dim), preferred_element_type=jnp.float32).astype(jnp.bfloat16)
             gate_pre = jnp.dot(rows, gate_ref[...], preferred_element_type=jnp.float32)
             up_pre = jnp.dot(rows, up_ref[...], preferred_element_type=jnp.float32)
             act = (jax.nn.silu(gate_pre) * up_pre).astype(jnp.bfloat16)
             for part, dy in ((3, 2), (1, 1), (2, -1), (0, 0)):
                 q = lax.rem(y + dy + tp_size, tp_size)
+                cols = pl.ds(pl.multiple_of(q * wide, wide), wide)
+                total = jnp.dot(act, down_ref[:, cols], preferred_element_type=jnp.float32).astype(jnp.bfloat16)
                 for d in (0, 1):
-                    cols = pl.ds(pl.multiple_of(q * wide + d * side, side), side)
-                    stage[s, part, d] = jnp.dot(act, down_ref[:, cols], preferred_element_type=jnp.float32).astype(jnp.bfloat16)
+                    stage[s, part, d] = total[:, d * side:(d + 1) * side]
             for d in (0, 1):
                 f_copy(s, d).start()
             for d in (0, 1):
                 d_copy(s, d).start()
 
-        @pl.when(i >= 2)
-        def _():
-            j = i - 2
+        @pl.when(i >= FINAL)
+        def _():
+            j = i - FINAL
             s = lax.rem(j, RING)
+            slot = lax.rem(j, FIN)
             tile = lax.rem(j, n_tiles)
             for d in (0, 1):
                 c_copy(s, d).wait_recv()
                 d_copy(s, d).wait_recv()
 
-            @pl.when((j >= RING) & (j < RING + n_tiles))
+            @pl.when((j >= FIN) & (j < FIN + n_tiles))
             def _():
-                own_copy(s, tile).wait()
-
-            @pl.when(j >= RING + n_tiles)
+                own_copy(slot, tile).wait()
+
+            @pl.when(j >= FIN + n_tiles)
             def _():
-                home_copy(2, s, tile).wait_send()
+                home_copy(2, slot, tile).wait_send()
 
             f32 = lambda a: a.astype(jnp.float32)
             for d in (0, 1):
                 total = f32(stage[s, 0, d]) + f32(recv_c[d, s]) + f32(recv_d[1 - d, s])
-                fin[s, :, d * side:(d + 1) * side] = total.astype(jnp.bfloat16)
+                fin[slot, :, d * side:(d + 1) * side] = total.astype(jnp.bfloat16)
 
             @pl.when(j < n_tiles)
             def _():
-                own_copy(s, tile).start()
+                own_copy(slot, tile).start()
 
             for k in range(1, len(BLOCKS)):
                 @pl.when(j // n_tiles == k)
                 def _(k=k):
-                    home_copy(k, s, tile).start()
-
-        @pl.when((i >= 1) & (i <= steps))
-        def _():
-            s = lax.rem(i - 1, RING)
+                    home_copy(k, slot, tile).start()
+
+        @pl.when((i >= CHAIN) & (i < steps + CHAIN))
+        def _():
+            s = lax.rem(i - CHAIN, RING)
             for d in (0, 1):
                 f_copy(s, d).wait_recv()
                 stage[s, 1 + d, d] = (stage[s, 1 + d, d].astype(jnp.float32) + recv_f[d, s].astype(jnp.float32)).astype(jnp.bfloat16)
@@ -276,14 +291,15 @@
 
         return carry
 
-    assert n_tiles == RING
-    lax.fori_loop(0, steps + 2, step, 0)
+    assert n_tiles == FIN
+    lax.fori_loop(0, steps + FINAL, step, 0)
 
     for s in range(RING):
         for d in (0, 1):
             f_copy(s, d).wait_send()
             c_copy(s, d).wait_send()
             d_copy(s, d).wait_send()
+    for s in range(FIN):
         home_copy(2, s, s).wait_send()
     for j in (0, 1):
         swap(j).wait_send()
@@ -319,13 +335,13 @@
         out_specs=(anywhere, anywhere),
         scratch_shapes=[
             pltpu.VMEM((dim, ff), bf16), pltpu.VMEM((dim, ff), bf16), pltpu.VMEM((ff, dim), bf16),
-            pltpu.VMEM(parts, bf16), pltpu.VMEM((1, tok_dev), jnp.int32),
+            pltpu.VMEM((2, *parts), bf16), pltpu.VMEM((2, 1, tok_dev), jnp.int32),
             pltpu.VMEM((RING, 4, 2, SLOT_TILE, side), bf16), pltpu.VMEM(ring, bf16), pltpu.VMEM(ring, bf16), pltpu.VMEM(ring, bf16),
-            pltpu.VMEM((RING, SLOT_TILE, width), bf16),
-            dma((3,)), dma, dma((2, 2)), dma((2, 2)), dma((2, 2)), dma((n,)), dma((n,)), dma((2, 2)), dma((2, 2)),
+            pltpu.VMEM((FIN, SLOT_TILE, width), bf16),
+            dma((3,)), dma((2,)), dma((2, 2)), dma((2, 2)), dma((2, 2)), dma((n,)), dma((n,)), dma((2, 2)), dma((2, 2)),
             dma((2, 2)), dma((2, 2)), dma((2, 2)), dma((2, 2)),
             dma((2, RING)), dma((2, RING)), dma((2, RING)), dma((2, RING)), dma((2, RING)), dma((2, RING)),
-            dma((RING,)), dma, dma((RING,)),
+            dma((FIN,)), dma, dma((FIN,)),
         ],
         cost_estimate=pl.CostEstimate(flops=2 * n * row_limit * dim * (tok_dev + 3 * ff), bytes_accessed=2 * (n * tok_dev * dim + 3 * dim * ff), transcendentals=n * row_limit * ff),
         compiler_params=pltpu.CompilerParams(collective_id=0, has_side_effects=True, vmem_limit_bytes=VMEM_LIMIT),

time: 521 us -> 495 us (0.950)
  Pallas kernels: 497 us -> 471 us
    pallas_call x1, Pallas kernels: 408 us -> 384 us  [experts_apply(): pl.pallas_call(functools.partial(expert_kernel, chips, tp_size), out_shap...]
where the time goes in v3:
time: 495 us
  Pallas kernels  471 us (95%)
  local copies, waits for them, and re-layouts  13.3 us (3%)
  starting transfers between devices  6.01 us (1%)
    pallas_call x1, Pallas kernels, experts_apply(): pl.pallas_call(functools.partial(expert_kernel, chips, tp_size), out_shap...  384 us
    pallas_call x1, Pallas kernels, finish(): pl.pallas_call(functools.partial(finish_kernel, tp_size), out_shape=jax.S...  78.4 us
    unnamed x7, local copies, waits for them, and re-layouts  10.1 us
  transfers between devices with their start and end apart: 1, of which 0 were waited for; matrix products, arithmetic and copies ran while one was open for 1% of the time, Pallas kernels for 2%

profile of v3, /device:TPU:97, one launch (start us, length us, event | category | flops | bytes accessed | tf_op | source)
XLA Modules:
  0.0 494.9 jit_solution(17752634964422317315)
XLA Ops:
  0.0 0.0 copy-start.1
  0.0 0.0 copy-start
  0.0 0.8 convert_reduce_fusion
  0.8 0.3 copy.30
  1.1 0.3 copy.31
  1.4 2.3 reduce-window.6
  3.7 0.3 slice_reduce_fusion
  4.0 0.2 reduce-window.9
  4.2 0.1 add_add_fusion
  4.2 0.3 copy.32
  4.6 0.1 bitcast_select_fusion.1
  4.7 0.9 copy.34
  5.6 6.0 %all-to-all-start = ((s32[8,1,2048]{2,1,0:T(1,128)}), s32[8,1,2048]{2,1,0:T(1,128)S(1)}, u32[]{:S(2)}, u32[]{:S(2)}) async-start(s32[8,1,2048]{2,1,0:T(1,128)} %copy.34), calls=%async_computation | async-start | bytes 131072 | tf_op jit(solution)/shard_map/all_to_all | solution.py:446
  11.7 0.4 copy.33
  12.1 1.1 bitcast_select_fusion.pos_ref
  13.2 0.0 copy-done.1
  13.2 0.6 reshape.25.w_ref
  13.8 0.0 copy-done
  13.8 1.0 copy.35.router_ref
  14.8 8.4 %norm_rows.1.v_hbm = bf16[2048,2048]{1,0:T(8,128)(2,1)} custom-call(bf16[2048,2048]{1,0:T(8,128)(2,1)} %hidden_hbm.1, bf16[1,2048]{1,0:T(2,128)(2,1)} %reshape.25.w_ref), custom_call_target="tpu_custom_call" | custom-call | flops 25165824 | bytes 16777216 | tf_op jit(solution)/shard_map/norm_rows/pallas_call | solution.py:39
  23.3 0.0 all-to-all-done
  23.3 0.6 copy.38
  23.9 384.1 %experts.1 = (bf16[7,4,2,256,2048]{4,3,2,1,0:T(8,128)(2,1)}, bf16[8,1024,512]{2,1,0:T(8,128)(2,1)}) custom-call(bf16[4,2,256,2048]{3,2,1,0:T(8,128)(2,1)} %bitcast.21, s32[8,2048]{1,0:T(8,128)} %bitcast.23, bf16[2048,1408]{1,0:T(8,128)(2,1)} %bitcast.25, bf16[2048,1408]{1,0:T(8,128)(2,1)} %bitcast.26, bf16[1408,2048]{1,0:T(8,128)(2,1)} %bitcast.27), custom_call_target="tpu_custom_call" | custom-call | flops 210453397504 | bytes 84410368 | tf_op jit(solution)/shard_map/experts/pallas_call | solution.py:331
  408.0 78.4 %finish.1 = bf16[2048,2048]{1,0:T(8,128)(2,1)} custom-call(s32[2048,8]{1,0:T(8,128)} %bitcast_select_fusion.pos_ref, bf16[2048,8]{1,0:T(8,128)(2,1)} %copy.35.router_ref, bf16[8,1024,512]{2,1,0:T(8,128)(2,1)} %get-tuple-element.6.y_ref, bf16[2048,2048]{1,0:T(8,128)(2,1)} %hidden_hbm.1, bf16[2048,2048]{1,0:T(8,128)(2,1)} %norm_rows.1.v_hbm), custom_call_target="tpu_custom_call" | custom-call | flops 17179869184 | bytes 16777216 | tf_op jit(solution)/shard_map/finish/pallas_call | solution.py:421
  486.4 8.4 %copy.40 = bf16[2048,2048]{1,0:T(8,128)(2,1)} copy(bf16[2048,2048]{1,0:T(8,128)(2,1)} %finish.1) | data formatting | bytes 16777216
  (1 shorter events, 0.0 us)
Async XLA Ops:
  0.0 13.2 %copy-start.1 = (bf16[2048]{0:T(1024)(128)(2,1)S(1)}, bf16[2048]{0:T(1024)(128)(2,1)}, u32[]{:S(2)}) copy-start(bf16[2048]{0:T(1024)(128)(2,1)} %param.9) | copy-start | bytes 12292
  0.0 13.8 %copy-start = (bf16[2048,8]{0,1:T(8,128)(2,1)S(1)}, bf16[2048,8]{0,1:T(8,128)(2,1)}, u32[]{:S(2)}) copy-start(bf16[2048,8]{0,1:T(8,128)(2,1)} %param.10) | copy-start | bytes 98308
  5.6 17.6 %all-to-all-start = ((s32[8,1,2048]{2,1,0:T(1,128)}), s32[8,1,2048]{2,1,0:T(1,128)S(1)}, u32[]{:S(2)}, u32[]{:S(2)}) async-start(s32[8,1,2048]{2,1,0:T(1,128)} %copy.34), calls=%async_computation | async-start | bytes 131072 | tf_op jit(solution)/shard_map/all_to_all | solution.py:446
